TPU v7x, 32 devices: a whole 2x2x4 slice. The times are simulated.
32 devices in a mesh: table: 4 (over y, core), batch: 8 (over z, x).
Axes of the slice: x: 2, y: 2, z: 4, core: 2. Of those that a mesh axis runs over, the one named last changes fastest.
Arguments:
- emb: bfloat16 [4, 262144, 128], P('table', 'batch'), may hold values from -6 to 6
- short_rows: int32 [192, 4, 32], P(('table', 'batch')), may hold values from 0 to 262143
- short_len: int32 [192, 4], P(('table', 'batch')), may hold values from 1 to 32
- short_sample: int32 [192, 4], P(('table', 'batch')), may hold values from 0 to 7, as said below
- long_rows: int32 [64, 4, 512], P(('table', 'batch')), may hold values from 0 to 262143, as said below
- long_len: int32 [64, 4], P(('table', 'batch')), may hold values from 33 to 500, as said below
- long_sample: int32 [64, 4], P(('table', 'batch')), may hold values from 0 to 7, as said below
Outputs:
- pooled: float32 [256, 4, 128], P(('table', 'batch'))
Inputs may be any that keep to these rules, and one draw needn't show every extreme that they name: For each block of 6 short bags and 2 long bags with the same j // 6 and j // 2, and each table, short_sample and long_sample together name each of the 8 samples exactly once. `long_sample`: see short_sample. `long_rows`: within one bag no row id stands more than 256 times among the first long_len positions, and in every draw some bag has a row id that stands exactly that often. `long_len`: in every draw some long bag has length 500.
All inputs are finite; a program needn't handle non-finite values.
Results may differ from a plain program's by a relative error of at most 0.0003.
Values sent between devices are 32-bit elements; how exact they have to be, the bound alone decides.
No kernel may reach another device: no remote copies, remote signals or barrier semaphores. Data moves between devices by JAX's collectives and lax.ppermute only.
A program may use at most 64 MiB of HBM per device.

v0:
```python
import jax
import jax.numpy as jnp
from jax import lax
from jax.sharding import PartitionSpec as P


def mask_rows(rows, lengths):
    place = lax.broadcasted_iota(jnp.int32, rows.shape, 2)
    return jnp.where(place < lengths[:, :, None], rows, -1)


def pool_rows(keys, table, row_base):
    bag_count = keys.shape[0]
    rows_dev = table.shape[0]
    block = min(8192, rows_dev)
    high_count = block // 128
    local = keys - row_base
    inside = (local >= 0) & (local < rows_dev)
    high = jnp.where(inside, local // 128, -1)
    low = jnp.where(inside, local % 128, -1)
    low_hot = (low[:, :, None] == lax.broadcasted_iota(jnp.int32, (1, 1, 128), 2)).astype(
        jnp.bfloat16
    )

    def add_block(index, total):
        targets = index * high_count + lax.broadcasted_iota(jnp.int32, (1, 1, high_count), 2)
        high_hot = (high[:, :, None] == targets).astype(jnp.bfloat16)
        counts = jnp.einsum("bwh,bwl->bhl", high_hot, low_hot, preferred_element_type=jnp.float32)
        counts = counts.astype(jnp.bfloat16).reshape(bag_count, block)
        piece = lax.dynamic_slice_in_dim(table, index * block, block, 0)
        return total + jnp.dot(counts, piece, preferred_element_type=jnp.float32)

    start = jnp.zeros((bag_count, table.shape[1]), jnp.float32)
    return lax.fori_loop(0, rows_dev // block, add_block, start)


def place_bags(values, lengths, samples, sample_count):
    scaled = values / jnp.sqrt(lengths.astype(jnp.float32))[:, :, None]
    slots = lax.broadcasted_iota(jnp.int32, samples.shape + (sample_count,), 2)
    picks = (samples[:, :, None] == slots).astype(jnp.float32)
    return jnp.sum(picks[:, :, :, None] * scaled[:, :, None, :], axis=0)


def on_device(emb, short_rows, short_len, short_sample, long_rows, long_len, long_sample):
    tab_dev = emb.shape[0]
    short_keys = mask_rows(short_rows, short_len)
    long_keys = mask_rows(long_rows, long_len)
    short_moved, long_moved = (
        lax.all_to_all(short_keys, "table", split_axis=1, concat_axis=0, tiled=True),
        lax.all_to_all(long_keys, "table", split_axis=1, concat_axis=0, tiled=True),
    )
    short_all, long_all = (
        lax.all_gather(short_moved, "batch", axis=0, tiled=True),
        lax.all_gather(long_moved, "batch", axis=0, tiled=True),
    )
    row_base = lax.axis_index("batch") * emb.shape[1]
    short_part = jnp.stack([pool_rows(short_all[:, 0, :], emb[0], row_base)], axis=1)
    long_part = jnp.stack([pool_rows(long_all[:, 0, :], emb[0], row_base)], axis=1)
    short_sum, long_sum = (
        lax.psum_scatter(short_part, "batch", scatter_dimension=0, tiled=True),
        lax.psum_scatter(long_part, "batch", scatter_dimension=0, tiled=True),
    )
    short_back, long_back = (
        lax.all_to_all(short_sum, "table", split_axis=0, concat_axis=1, tiled=True),
        lax.all_to_all(long_sum, "table", split_axis=0, concat_axis=1, tiled=True),
    )
    sample_count = short_sample.shape[0] + long_sample.shape[0]
    pooled = place_bags(short_back, short_len, short_sample, sample_count)
    pooled = pooled + place_bags(long_back, long_len, long_sample, sample_count)
    return jnp.transpose(pooled, (1, 0, 2))


def solution(mesh):
    return jax.shard_map(
        on_device,
        mesh=mesh,
        in_specs=(
            P("table", "batch", None),
            P(("table", "batch"), None, None),
            P(("table", "batch"), None),
            P(("table", "batch"), None),
            P(("table", "batch"), None, None),
            P(("table", "batch"), None),
            P(("table", "batch"), None),
        ),
        out_specs=P(("table", "batch"), None, None),
        check_vma=False,
    )
```

profile of v0, /device:TPU:0, one launch (start us, length us, event | category | flops | bytes accessed | tf_op | source)
XLA Modules:
  0.0 266.0 jit_solution(12417706467865206309)
XLA Ops:
  6.5 0.8 fusion.56
  8.0 4.3 %all-to-all-start = ((s32[4,1,192]{2,1,0:T(1,128)}), s32[4,1,192]{2,1,0:T(1,128)S(1)}, u32[]{:S(2)}, u32[]{:S(2)}) async-start(s32[4,1,192]{2,1,0:T(1,128)} %reshape.94), calls=%async_computation | async-start | bytes 8192 | tf_op jit(solution)/shard_map/all_to_all | solution.py:49
  12.9 0.8 copy.38
  13.8 0.8 copy.42
  15.3 1.4 compare_select_fusion
  17.5 1.3 dynamic-slice
  19.4 3.3 %all-to-all-start.2 = ((s32[2,4,512]{2,0,1:T(2,128)}), s32[2,4,512]{2,0,1:T(2,128)S(1)}, u32[]{:S(2)}, u32[]{:S(2)}) async-start(s32[2,4,512]{2,0,1:T(2,128)} %compare_select_fusion), calls=%async_computation.2 | async-start | bytes 32768 | tf_op jit(solution)/shard_map/all_to_all | solution.py:50
  24.0 31.3 %all_gather.6 = s32[192,1,32]{2,1,0:T(1,128)S(1)} all-gather(s32[24,1,32]{2,1,0:T(1,128)S(1)} %all_to_all.51), channel_id=1, replica_groups=mesh['table'=4,'batch'=8] {'batch'}, dimensions={0}, use_global_device_ids=true | all-gather | bytes 27648 | tf_op jit(solution)/shard_map/all_gather | solution.py:53
  55.4 30.5 %all_gather.7 = s32[64,1,512]{2,0,1:T(8,128)S(1)} all-gather(s32[8,1,512]{2,0,1:T(8,128)S(1)} %all_to_all.58), channel_id=1, replica_groups=mesh['table'=4,'batch'=8] {'batch'}, dimensions={0}, use_global_device_ids=true | all-gather | bytes 147456 | tf_op jit(solution)/shard_map/all_gather | solution.py:54
  86.1 31.9 %while.29 = (s32[]{:T(128)}, f32[64,128]{1,0:T(8,128)S(1)}, s32[64,512]{1,0:T(8,128)S(1)}, bf16[32768,128]{1,0:T(8,128)(2,1)}, s32[64,512]{1,0:T(8,128)S(1)}, /*...) while((s32[]{:T(128)}, f32[64,128]{1,0:T(8,128)S(1)}, s32[64,512]{1,0:T(8,128)S(1)}, ...), condition=%wide.region_5.6_spmd.clone, body=%wide.region_4.5_spmd.clone.sunk | while | flops 682115136 | bytes 4522681 | solution.py:34
  86.1 5.5 %fusion.79 = bf16[64,64,128]{2,1,0:T(8,128)(2,1)S(1)} fusion(s32[64,512]{1,0:T(8,128)S(1)} %get-tuple-element.377, s32[64,512]{1,0:T(8,128)S(1)} %get-tuple-element.375, s32[64]{0:T(128)S(1)} %iota_add_fusion.5), kind=kOutput, calls=%fused_computation.26.clone.1 | convolution fusion | flops 547880960 | bytes 1310976 | tf_op jit(solution)/shard_map/while/body/eval_jaxpr/bwh,bwl->bhl/dot_general | solution.py:28
  91.6 2.4 fusion.80
  94.1 5.5 %fusion.79 = bf16[64,64,128]{2,1,0:T(8,128)(2,1)S(1)} fusion(s32[64,512]{1,0:T(8,128)S(1)} %get-tuple-element.377, s32[64,512]{1,0:T(8,128)S(1)} %get-tuple-element.375, s32[64]{0:T(128)S(1)} %iota_add_fusion.5), kind=kOutput, calls=%fused_computation.26.clone.1 | convolution fusion | flops 547880960 | bytes 1310976 | tf_op jit(solution)/shard_map/while/body/eval_jaxpr/bwh,bwl->bhl/dot_general | solution.py:28
  99.6 2.4 fusion.80
  102.1 5.5 %fusion.79 = bf16[64,64,128]{2,1,0:T(8,128)(2,1)S(1)} fusion(s32[64,512]{1,0:T(8,128)S(1)} %get-tuple-element.377, s32[64,512]{1,0:T(8,128)S(1)} %get-tuple-element.375, s32[64]{0:T(128)S(1)} %iota_add_fusion.5), kind=kOutput, calls=%fused_computation.26.clone.1 | convolution fusion | flops 547880960 | bytes 1310976 | tf_op jit(solution)/shard_map/while/body/eval_jaxpr/bwh,bwl->bhl/dot_general | solution.py:28
  107.6 2.4 fusion.80
  110.1 5.5 %fusion.79 = bf16[64,64,128]{2,1,0:T(8,128)(2,1)S(1)} fusion(s32[64,512]{1,0:T(8,128)S(1)} %get-tuple-element.377, s32[64,512]{1,0:T(8,128)S(1)} %get-tuple-element.375, s32[64]{0:T(128)S(1)} %iota_add_fusion.5), kind=kOutput, calls=%fused_computation.26.clone.1 | convolution fusion | flops 547880960 | bytes 1310976 | tf_op jit(solution)/shard_map/while/body/eval_jaxpr/bwh,bwl->bhl/dot_general | solution.py:28
  115.6 2.4 fusion.80
  118.0 37.0 %all-reduce.1 = f32[64,1,128]{2,0,1:T(8,128)S(1)} all-reduce(f32[64,1,128]{2,0,1:T(8,128)S(1)} %bitcast.97), channel_id=3, replica_groups=mesh['table'=4,'batch'=8] {'batch'}, use_global_device_ids=true, to_apply=%region_6.7.clone | all-reduce | flops 8192 | bytes 65536
  155.7 3.3 %all-to-all-start.3 = ((f32[8,1,128]{2,1,0:T(1,128)}), f32[8,1,128]{2,1,0:T(1,128)S(1)}, u32[]{:S(2)}, u32[]{:S(2)}) async-start(f32[8,1,128]{2,1,0:T(1,128)} %bitcast.13), calls=%async_computation.3 | async-start | bytes 8192 | tf_op jit(solution)/shard_map/all_to_all | solution.py:65
  159.0 35.0 %while.28 = (s32[]{:T(128)}, f32[192,128]{1,0:T(8,128)S(1)}, s32[192,32]{1,0:T(8,128)S(1)}, bf16[32768,128]{1,0:T(8,128)(2,1)}, s32[192,32]{1,0:T(8,128)S(1)}, /...) while((s32[]{:T(128)}, f32[192,128]{1,0:T(8,128)S(1)}, s32[192,32]{1,0:T(8,128)S(1)}, ...), condition=%wide.region_1.2_spmd.clone, body=%wide.region_0.1_spmd.clone.sunk | while | flops 506904640 | bytes 8635065 | solution.py:34
  159.0 5.1 %fusion.73 = bf16[192,64,128]{2,1,0:T(8,128)(2,1)S(1)} fusion(s32[192,32]{1,0:T(8,128)S(1)} %get-tuple-element.347, s32[64]{0:T(128)S(1)} %iota_add_fusion.4, s32[192,32]{1,0:T(8,128)S(1)} %get-tuple-element.345), kind=kOutput, calls=%fused_computation.9.clone.1 | convolution fusion | flops 104202240 | bytes 3195136 | tf_op jit(solution)/shard_map/while/body/eval_jaxpr/bwh,bwl->bhl/dot_general | solution.py:28
  164.1 3.6 %fusion.74 = f32[192,128]{1,0:T(8,128)S(1)} fusion(bf16[32768,128]{1,0:T(8,128)(2,1)} %get-tuple-element.346, s32[]{:T(128)S(6)} %select_n.109, bf16[24,8,64,128]{3,2,1,0:T(8,128)(2,1)S(1)} %bitcast.106, f32[192,128]{1,0:T(8,128)S(1)} %get-tuple-element.334, pred[]{:T(512)S(6)} %compare.18), kind=kOutput, calls=%fused_computation.14.clone.1 | convolution fusion | flops 402702336 | bytes 5439493 | tf_op jit(solution)/shard_map/while/body/eval_jaxpr/dot_general | solution.py:31
  167.7 5.1 %fusion.73 = bf16[192,64,128]{2,1,0:T(8,128)(2,1)S(1)} fusion(s32[192,32]{1,0:T(8,128)S(1)} %get-tuple-element.347, s32[64]{0:T(128)S(1)} %iota_add_fusion.4, s32[192,32]{1,0:T(8,128)S(1)} %get-tuple-element.345), kind=kOutput, calls=%fused_computation.9.clone.1 | convolution fusion | flops 104202240 | bytes 3195136 | tf_op jit(solution)/shard_map/while/body/eval_jaxpr/bwh,bwl->bhl/dot_general | solution.py:28
  172.8 3.6 %fusion.74 = f32[192,128]{1,0:T(8,128)S(1)} fusion(bf16[32768,128]{1,0:T(8,128)(2,1)} %get-tuple-element.346, s32[]{:T(128)S(6)} %select_n.109, bf16[24,8,64,128]{3,2,1,0:T(8,128)(2,1)S(1)} %bitcast.106, f32[192,128]{1,0:T(8,128)S(1)} %get-tuple-element.334, pred[]{:T(512)S(6)} %compare.18), kind=kOutput, calls=%fused_computation.14.clone.1 | convolution fusion | flops 402702336 | bytes 5439493 | tf_op jit(solution)/shard_map/while/body/eval_jaxpr/dot_general | solution.py:31
  176.5 5.1 %fusion.73 = bf16[192,64,128]{2,1,0:T(8,128)(2,1)S(1)} fusion(s32[192,32]{1,0:T(8,128)S(1)} %get-tuple-element.347, s32[64]{0:T(128)S(1)} %iota_add_fusion.4, s32[192,32]{1,0:T(8,128)S(1)} %get-tuple-element.345), kind=kOutput, calls=%fused_computation.9.clone.1 | convolution fusion | flops 104202240 | bytes 3195136 | tf_op jit(solution)/shard_map/while/body/eval_jaxpr/bwh,bwl->bhl/dot_general | solution.py:28
  181.6 3.6 %fusion.74 = f32[192,128]{1,0:T(8,128)S(1)} fusion(bf16[32768,128]{1,0:T(8,128)(2,1)} %get-tuple-element.346, s32[]{:T(128)S(6)} %select_n.109, bf16[24,8,64,128]{3,2,1,0:T(8,128)(2,1)S(1)} %bitcast.106, f32[192,128]{1,0:T(8,128)S(1)} %get-tuple-element.334, pred[]{:T(512)S(6)} %compare.18), kind=kOutput, calls=%fused_computation.14.clone.1 | convolution fusion | flops 402702336 | bytes 5439493 | tf_op jit(solution)/shard_map/while/body/eval_jaxpr/dot_general | solution.py:31
  185.2 5.1 %fusion.73 = bf16[192,64,128]{2,1,0:T(8,128)(2,1)S(1)} fusion(s32[192,32]{1,0:T(8,128)S(1)} %get-tuple-element.347, s32[64]{0:T(128)S(1)} %iota_add_fusion.4, s32[192,32]{1,0:T(8,128)S(1)} %get-tuple-element.345), kind=kOutput, calls=%fused_computation.9.clone.1 | convolution fusion | flops 104202240 | bytes 3195136 | tf_op jit(solution)/shard_map/while/body/eval_jaxpr/bwh,bwl->bhl/dot_general | solution.py:28
  190.3 3.6 %fusion.74 = f32[192,128]{1,0:T(8,128)S(1)} fusion(bf16[32768,128]{1,0:T(8,128)(2,1)} %get-tuple-element.346, s32[]{:T(128)S(6)} %select_n.109, bf16[24,8,64,128]{3,2,1,0:T(8,128)(2,1)S(1)} %bitcast.106, f32[192,128]{1,0:T(8,128)S(1)} %get-tuple-element.334, pred[]{:T(512)S(6)} %compare.18), kind=kOutput, calls=%fused_computation.14.clone.1 | convolution fusion | flops 402702336 | bytes 5439493 | tf_op jit(solution)/shard_map/while/body/eval_jaxpr/dot_general | solution.py:31
  194.7 56.6 %reduce-scatter.6.cloned.1.call-done = f32[24,1,128]{2,0,1:T(8,128)} async-done(((f32[192,1,128]{2,0,1:T(8,128)}), f32[24,1,128]{2,0,1:T(8,128)}) %reduce-scatter.6.cloned.1.call-update) | async-done | bytes 12304
  251.3 3.2 %all-to-all-start.1 = ((f32[24,1,128]{2,1,0:T(1,128)}), f32[24,1,128]{2,1,0:T(1,128)S(1)}, u32[]{:S(2)}, u32[]{:S(2)}) async-start(f32[24,1,128]{2,1,0:T(1,128)} %bitcast.105), calls=%async_computation.1 | async-start | bytes 24576 | tf_op jit(solution)/shard_map/all_to_all | solution.py:64
  254.6 3.7 %all-to-all-done.1 = f32[24,1,128]{2,1,0:T(1,128)S(1)} async-done(((f32[24,1,128]{2,1,0:T(1,128)}), f32[24,1,128]{2,1,0:T(1,128)S(1)}, u32[]{:S(2)}, u32[]{:S(2)}) %all-to-all-start.1) | async-done | bytes 12320 | tf_op jit(solution)/shard_map/all_to_all | solution.py:64
  (41 shorter events, 6.7 us)
Async XLA Ops:
  8.0 11.4 %all-to-all-start = ((s32[4,1,192]{2,1,0:T(1,128)}), s32[4,1,192]{2,1,0:T(1,128)S(1)}, u32[]{:S(2)}, u32[]{:S(2)}) async-start(s32[4,1,192]{2,1,0:T(1,128)} %reshape.94), calls=%async_computation | async-start | bytes 8192 | tf_op jit(solution)/shard_map/all_to_all | solution.py:49
  19.4 36.0 %all-to-all-start.2 = ((s32[2,4,512]{2,0,1:T(2,128)}), s32[2,4,512]{2,0,1:T(2,128)S(1)}, u32[]{:S(2)}, u32[]{:S(2)}) async-start(s32[2,4,512]{2,0,1:T(2,128)} %compare_select_fusion), calls=%async_computation.2 | async-start | bytes 32768 | tf_op jit(solution)/shard_map/all_to_all | solution.py:50
  155.7 39.0 %all-to-all-start.3 = ((f32[8,1,128]{2,1,0:T(1,128)}), f32[8,1,128]{2,1,0:T(1,128)S(1)}, u32[]{:S(2)}, u32[]{:S(2)}) async-start(f32[8,1,128]{2,1,0:T(1,128)} %bitcast.13), calls=%async_computation.3 | async-start | bytes 8192 | tf_op jit(solution)/shard_map/all_to_all | solution.py:65
  158.9 92.3 %reduce-scatter.6.cloned.1.call-start = ((), (), s32[]{:S(2)}) async-start(), calls=%async_computation.5 | async-start | bytes 110592
  194.0 0.6 copy-start
  251.3 7.0 %all-to-all-start.1 = ((f32[24,1,128]{2,1,0:T(1,128)}), f32[24,1,128]{2,1,0:T(1,128)S(1)}, u32[]{:S(2)}, u32[]{:S(2)}) async-start(f32[24,1,128]{2,1,0:T(1,128)} %bitcast.105), calls=%async_computation.1 | async-start | bytes 24576 | tf_op jit(solution)/shard_map/all_to_all | solution.py:64
Sparse Core Ops, SparseCore 0:
  194.7 56.4 reduce-scatter.5
where the time goes:
time: 267 us; the launch traced here: 266 us
  blocking collectives  98.9 us (37%)
  matrix products  66.5 us (25%)
  waiting for transfers between devices  60.3 us (23%)
  starting transfers between devices  14.1 us (5%)
  between operations  14.1 us (5%)
  local copies, waits for them, and re-layouts  6.04 us (2%)
  other arithmetic  5.64 us (2%)
    unnamed x2, waiting for transfers between devices  56.6 us
    dot_general x8, matrix products, add_block(): jnp.einsum('bwh,bwl->bhl', high_hot, low_hot, preferred_element_type=jnp....  42.2 us
    unnamed x1, blocking collectives  37 us
    all_gather x1, blocking collectives, on_device(): lax.all_gather(short_moved, 'batch', axis=0, tiled=True)  31.3 us
    all_gather x1, blocking collectives, on_device(): lax.all_gather(long_moved, 'batch', axis=0, tiled=True)  30.5 us
    dot_general x8, matrix products, add_block(): return total + jnp.dot(counts, piece, preferred_element_type=jnp.float32)  24.3 us
  transfers between devices with their start and end apart: 5, of which 2 were waited for; matrix products, arithmetic and copies ran while one was open for 16% of the time, Pallas kernels for 0%

commit v1 on v0

--- a/solution.py
+++ b/solution.py
@@ -50,7 +50,9 @@
         lax.all_to_all(long_keys, "table", split_axis=1, concat_axis=0, tiled=True),
     )
     short_all, long_all = (
-        lax.all_gather(short_moved, "batch", axis=0, tiled=True),
+        jnp.concatenate(
+            lax.all_to_all(jnp.stack([short_moved] * lax.axis_size("batch")), "batch", 0, 0), axis=0
+        ),
         lax.all_gather(long_moved, "batch", axis=0, tiled=True),
     )
     row_base = lax.axis_index("batch") * emb.shape[1]

time: 267 us -> 245 us (0.918)
  blocking collectives: 98.9 us -> 68.1 us
  starting transfers between devices: 14.1 us -> 20.3 us
    all_gather x1 -> x0, blocking collectives: 31.3 us -> none  [on_device(): lax.all_gather(short_moved, 'batch', axis=0, tiled=True)]
    all_to_all x0 -> x1, starting transfers between devices: none -> 6.21 us  [on_device(): lax.all_to_all(jnp.stack([short_moved] * lax.axis_size('batch')), 'batch'...]
    unnamed x8 -> x11, local copies, waits for them, and re-layouts: 4.75 us -> 5.58 us
  transfers between devices with their start and end apart: 5 -> 6, of which waited for: 2 -> 3; matrix products, arithmetic and copies ran while one was open for 16% -> 31% of each run, Pallas kernels for 0% -> 0%
where the time goes in v1:
time: 245 us
  blocking collectives  68.1 us (28%)
  matrix products  66.3 us (27%)
  waiting for transfers between devices  62.1 us (25%)
  starting transfers between devices  20.3 us (8%)
  between operations  14.2 us (6%)
  local copies, waits for them, and re-layouts  6.86 us (3%)
  other arithmetic  6.28 us (3%)
    unnamed x2, waiting for transfers between devices  56.5 us
    dot_general x8, matrix products, add_block(): jnp.einsum('bwh,bwl->bhl', high_hot, low_hot, preferred_element_type=jnp....  42.2 us
    unnamed x1, blocking collectives  37 us
    all_gather x1, blocking collectives, on_device(): lax.all_gather(long_moved, 'batch', axis=0, tiled=True)  31.1 us
    dot_general x8, matrix products, add_block(): return total + jnp.dot(counts, piece, preferred_element_type=jnp.float32)  24.1 us
    all_to_all x1, starting transfers between devices, on_device(): lax.all_to_all(jnp.stack([short_moved] * lax.axis_size('batch')), 'batch'...  6.21 us
    unnamed x11, local copies, waits for them, and re-layouts  5.58 us
  transfers between devices with their start and end apart: 6, of which 3 were waited for; matrix products, arithmetic and copies ran while one was open for 31% of the time, Pallas kernels for 0%

profile of v1, /device:TPU:0, one launch (start us, length us, event | category | flops | bytes accessed | tf_op | source)
XLA Modules:
  0.0 244.6 jit_solution(17174562413746912792)
XLA Ops:
  6.5 0.8 fusion.58
  8.0 4.3 %all-to-all-start = ((s32[4,1,192]{2,1,0:T(1,128)}), s32[4,1,192]{2,1,0:T(1,128)S(1)}, u32[]{:S(2)}, u32[]{:S(2)}) async-start(s32[4,1,192]{2,1,0:T(1,128)} %reshape.99), calls=%async_computation | async-start | bytes 8192 | tf_op jit(solution)/shard_map/all_to_all | solution.py:49
  12.9 0.8 copy.37
  15.3 1.4 compare_select_fusion
  17.5 1.3 dynamic-slice
  19.4 3.3 %all-to-all-start.3 = ((s32[2,4,512]{2,0,1:T(2,128)}), s32[2,4,512]{2,0,1:T(2,128)S(1)}, u32[]{:S(2)}, u32[]{:S(2)}) async-start(s32[2,4,512]{2,0,1:T(2,128)} %compare_select_fusion), calls=%async_computation.3 | async-start | bytes 32768 | tf_op jit(solution)/shard_map/all_to_all | solution.py:50
  24.7 1.9 all-to-all-done.3
  26.6 6.2 %all-to-all-start.1 = ((s32[8,1,768]{2,1,0:T(1,128)}), s32[8,1,768]{2,1,0:T(1,128)S(1)}, u32[]{:S(2)}, u32[]{:S(2)}) async-start(s32[8,1,768]{2,1,0:T(1,128)} %reshape.101), calls=%async_computation.1 | async-start | bytes 49152 | tf_op jit(solution)/shard_map/all_to_all | solution.py:54
  32.8 31.1 %all_gather.3 = s32[64,1,512]{2,0,1:T(8,128)S(1)} all-gather(s32[8,1,512]{2,0,1:T(8,128)S(1)} %all_to_all.59), channel_id=1, replica_groups=mesh['table'=4,'batch'=8] {'batch'}, dimensions={0}, use_global_device_ids=true | all-gather | bytes 147456 | tf_op jit(solution)/shard_map/all_gather | solution.py:56
  64.0 31.7 %while.29 = (s32[]{:T(128)}, f32[64,128]{1,0:T(8,128)S(1)}, s32[64,512]{1,0:T(8,128)S(1)}, bf16[32768,128]{1,0:T(8,128)(2,1)}, s32[64,512]{1,0:T(8,128)S(1)}, /*...) while((s32[]{:T(128)}, f32[64,128]{1,0:T(8,128)S(1)}, s32[64,512]{1,0:T(8,128)S(1)}, ...), condition=%wide.region_5.6_spmd.clone, body=%wide.region_4.5_spmd.clone.sunk | while | flops 682115136 | bytes 4522673 | solution.py:34
  64.0 5.5 %fusion.81 = bf16[64,64,128]{2,1,0:T(8,128)(2,1)S(1)} fusion(s32[64,512]{1,0:T(8,128)S(1)} %get-tuple-element.377, s32[64,512]{1,0:T(8,128)S(1)} %get-tuple-element.375, s32[64]{0:T(128)S(1)} %iota_add_fusion.5), kind=kOutput, calls=%fused_computation.26.clone.1 | convolution fusion | flops 547880960 | bytes 1310976 | tf_op jit(solution)/shard_map/while/body/eval_jaxpr/bwh,bwl->bhl/dot_general | solution.py:28
  69.5 2.4 fusion.82
  72.0 5.5 %fusion.81 = bf16[64,64,128]{2,1,0:T(8,128)(2,1)S(1)} fusion(s32[64,512]{1,0:T(8,128)S(1)} %get-tuple-element.377, s32[64,512]{1,0:T(8,128)S(1)} %get-tuple-element.375, s32[64]{0:T(128)S(1)} %iota_add_fusion.5), kind=kOutput, calls=%fused_computation.26.clone.1 | convolution fusion | flops 547880960 | bytes 1310976 | tf_op jit(solution)/shard_map/while/body/eval_jaxpr/bwh,bwl->bhl/dot_general | solution.py:28
  77.5 2.4 fusion.82
  79.9 5.5 %fusion.81 = bf16[64,64,128]{2,1,0:T(8,128)(2,1)S(1)} fusion(s32[64,512]{1,0:T(8,128)S(1)} %get-tuple-element.377, s32[64,512]{1,0:T(8,128)S(1)} %get-tuple-element.375, s32[64]{0:T(128)S(1)} %iota_add_fusion.5), kind=kOutput, calls=%fused_computation.26.clone.1 | convolution fusion | flops 547880960 | bytes 1310976 | tf_op jit(solution)/shard_map/while/body/eval_jaxpr/bwh,bwl->bhl/dot_general | solution.py:28
  85.4 2.4 fusion.82
  87.8 5.5 %fusion.81 = bf16[64,64,128]{2,1,0:T(8,128)(2,1)S(1)} fusion(s32[64,512]{1,0:T(8,128)S(1)} %get-tuple-element.377, s32[64,512]{1,0:T(8,128)S(1)} %get-tuple-element.375, s32[64]{0:T(128)S(1)} %iota_add_fusion.5), kind=kOutput, calls=%fused_computation.26.clone.1 | convolution fusion | flops 547880960 | bytes 1310976 | tf_op jit(solution)/shard_map/while/body/eval_jaxpr/bwh,bwl->bhl/dot_general | solution.py:28
  93.3 2.4 fusion.82
  95.7 37.0 %all-reduce.1 = f32[64,1,128]{2,0,1:T(8,128)S(1)} all-reduce(f32[64,1,128]{2,0,1:T(8,128)S(1)} %bitcast.134), channel_id=3, replica_groups=mesh['table'=4,'batch'=8] {'batch'}, use_global_device_ids=true, to_apply=%region_6.7.clone | all-reduce | flops 8192 | bytes 65536
  133.4 3.2 %all-to-all-start.4 = ((f32[8,1,128]{2,1,0:T(1,128)}), f32[8,1,128]{2,1,0:T(1,128)S(1)}, u32[]{:S(2)}, u32[]{:S(2)}) async-start(f32[8,1,128]{2,1,0:T(1,128)} %bitcast.13), calls=%async_computation.4 | async-start | bytes 8192 | tf_op jit(solution)/shard_map/all_to_all | solution.py:67
  137.6 35.0 %while.28 = (s32[]{:T(128)}, f32[192,128]{1,0:T(8,128)S(1)}, s32[192,32]{1,0:T(8,128)S(1)}, bf16[32768,128]{1,0:T(8,128)(2,1)}, s32[192,32]{1,0:T(8,128)S(1)}, /...) while((s32[]{:T(128)}, f32[192,128]{1,0:T(8,128)S(1)}, s32[192,32]{1,0:T(8,128)S(1)}, ...), condition=%wide.region_1.2_spmd.clone, body=%wide.region_0.1_spmd.clone.sunk | while | flops 506904640 | bytes 8635057 | solution.py:34
  137.6 5.1 %fusion.75 = bf16[192,64,128]{2,1,0:T(8,128)(2,1)S(1)} fusion(s32[192,32]{1,0:T(8,128)S(1)} %get-tuple-element.347, s32[64]{0:T(128)S(1)} %iota_add_fusion.4, s32[192,32]{1,0:T(8,128)S(1)} %get-tuple-element.345), kind=kOutput, calls=%fused_computation.9.clone.1 | convolution fusion | flops 104202240 | bytes 3195136 | tf_op jit(solution)/shard_map/while/body/eval_jaxpr/bwh,bwl->bhl/dot_general | solution.py:28
  142.7 3.6 %fusion.76 = f32[192,128]{1,0:T(8,128)S(1)} fusion(bf16[32768,128]{1,0:T(8,128)(2,1)} %get-tuple-element.346, s32[]{:T(128)S(6)} %select_n.109, bf16[24,8,64,128]{3,2,1,0:T(8,128)(2,1)S(1)} %bitcast.141, f32[192,128]{1,0:T(8,128)S(1)} %get-tuple-element.334, pred[]{:T(512)S(6)} %compare.18), kind=kOutput, calls=%fused_computation.14.clone.1 | convolution fusion | flops 402702336 | bytes 5439493 | tf_op jit(solution)/shard_map/while/body/eval_jaxpr/dot_general | solution.py:31
  146.3 5.1 %fusion.75 = bf16[192,64,128]{2,1,0:T(8,128)(2,1)S(1)} fusion(s32[192,32]{1,0:T(8,128)S(1)} %get-tuple-element.347, s32[64]{0:T(128)S(1)} %iota_add_fusion.4, s32[192,32]{1,0:T(8,128)S(1)} %get-tuple-element.345), kind=kOutput, calls=%fused_computation.9.clone.1 | convolution fusion | flops 104202240 | bytes 3195136 | tf_op jit(solution)/shard_map/while/body/eval_jaxpr/bwh,bwl->bhl/dot_general | solution.py:28
  151.4 3.6 %fusion.76 = f32[192,128]{1,0:T(8,128)S(1)} fusion(bf16[32768,128]{1,0:T(8,128)(2,1)} %get-tuple-element.346, s32[]{:T(128)S(6)} %select_n.109, bf16[24,8,64,128]{3,2,1,0:T(8,128)(2,1)S(1)} %bitcast.141, f32[192,128]{1,0:T(8,128)S(1)} %get-tuple-element.334, pred[]{:T(512)S(6)} %compare.18), kind=kOutput, calls=%fused_computation.14.clone.1 | convolution fusion | flops 402702336 | bytes 5439493 | tf_op jit(solution)/shard_map/while/body/eval_jaxpr/dot_general | solution.py:31
  155.1 5.1 %fusion.75 = bf16[192,64,128]{2,1,0:T(8,128)(2,1)S(1)} fusion(s32[192,32]{1,0:T(8,128)S(1)} %get-tuple-element.347, s32[64]{0:T(128)S(1)} %iota_add_fusion.4, s32[192,32]{1,0:T(8,128)S(1)} %get-tuple-element.345), kind=kOutput, calls=%fused_computation.9.clone.1 | convolution fusion | flops 104202240 | bytes 3195136 | tf_op jit(solution)/shard_map/while/body/eval_jaxpr/bwh,bwl->bhl/dot_general | solution.py:28
  160.2 3.6 %fusion.76 = f32[192,128]{1,0:T(8,128)S(1)} fusion(bf16[32768,128]{1,0:T(8,128)(2,1)} %get-tuple-element.346, s32[]{:T(128)S(6)} %select_n.109, bf16[24,8,64,128]{3,2,1,0:T(8,128)(2,1)S(1)} %bitcast.141, f32[192,128]{1,0:T(8,128)S(1)} %get-tuple-element.334, pred[]{:T(512)S(6)} %compare.18), kind=kOutput, calls=%fused_computation.14.clone.1 | convolution fusion | flops 402702336 | bytes 5439493 | tf_op jit(solution)/shard_map/while/body/eval_jaxpr/dot_general | solution.py:31
  163.8 5.1 %fusion.75 = bf16[192,64,128]{2,1,0:T(8,128)(2,1)S(1)} fusion(s32[192,32]{1,0:T(8,128)S(1)} %get-tuple-element.347, s32[64]{0:T(128)S(1)} %iota_add_fusion.4, s32[192,32]{1,0:T(8,128)S(1)} %get-tuple-element.345), kind=kOutput, calls=%fused_computation.9.clone.1 | convolution fusion | flops 104202240 | bytes 3195136 | tf_op jit(solution)/shard_map/while/body/eval_jaxpr/bwh,bwl->bhl/dot_general | solution.py:28
  168.9 3.6 %fusion.76 = f32[192,128]{1,0:T(8,128)S(1)} fusion(bf16[32768,128]{1,0:T(8,128)(2,1)} %get-tuple-element.346, s32[]{:T(128)S(6)} %select_n.109, bf16[24,8,64,128]{3,2,1,0:T(8,128)(2,1)S(1)} %bitcast.141, f32[192,128]{1,0:T(8,128)S(1)} %get-tuple-element.334, pred[]{:T(512)S(6)} %compare.18), kind=kOutput, calls=%fused_computation.14.clone.1 | convolution fusion | flops 402702336 | bytes 5439493 | tf_op jit(solution)/shard_map/while/body/eval_jaxpr/dot_general | solution.py:31
  173.3 56.5 %reduce-scatter.6.cloned.1.call-done = f32[24,1,128]{2,0,1:T(8,128)} async-done(((f32[192,1,128]{2,0,1:T(8,128)}), f32[24,1,128]{2,0,1:T(8,128)}) %reduce-scatter.6.cloned.1.call-update) | async-done | bytes 12304
  229.8 3.2 %all-to-all-start.2 = ((f32[24,1,128]{2,1,0:T(1,128)}), f32[24,1,128]{2,1,0:T(1,128)S(1)}, u32[]{:S(2)}, u32[]{:S(2)}) async-start(f32[24,1,128]{2,1,0:T(1,128)} %bitcast.140), calls=%async_computation.2 | async-start | bytes 24576 | tf_op jit(solution)/shard_map/all_to_all | solution.py:66
  233.2 3.7 %all-to-all-done.2 = f32[24,1,128]{2,1,0:T(1,128)S(1)} async-done(((f32[24,1,128]{2,1,0:T(1,128)}), f32[24,1,128]{2,1,0:T(1,128)S(1)}, u32[]{:S(2)}, u32[]{:S(2)}) %all-to-all-start.2) | async-done | bytes 12320 | tf_op jit(solution)/shard_map/all_to_all | solution.py:66
  (46 shorter events, 9.0 us)
Async XLA Ops:
  8.0 11.4 %all-to-all-start = ((s32[4,1,192]{2,1,0:T(1,128)}), s32[4,1,192]{2,1,0:T(1,128)S(1)}, u32[]{:S(2)}, u32[]{:S(2)}) async-start(s32[4,1,192]{2,1,0:T(1,128)} %reshape.99), calls=%async_computation | async-start | bytes 8192 | tf_op jit(solution)/shard_map/all_to_all | solution.py:49
  19.4 7.2 %all-to-all-start.3 = ((s32[2,4,512]{2,0,1:T(2,128)}), s32[2,4,512]{2,0,1:T(2,128)S(1)}, u32[]{:S(2)}, u32[]{:S(2)}) async-start(s32[2,4,512]{2,0,1:T(2,128)} %compare_select_fusion), calls=%async_computation.3 | async-start | bytes 32768 | tf_op jit(solution)/shard_map/all_to_all | solution.py:50
  26.6 106.8 %all-to-all-start.1 = ((s32[8,1,768]{2,1,0:T(1,128)}), s32[8,1,768]{2,1,0:T(1,128)S(1)}, u32[]{:S(2)}, u32[]{:S(2)}) async-start(s32[8,1,768]{2,1,0:T(1,128)} %reshape.101), calls=%async_computation.1 | async-start | bytes 49152 | tf_op jit(solution)/shard_map/all_to_all | solution.py:54
  133.4 39.9 %all-to-all-start.4 = ((f32[8,1,128]{2,1,0:T(1,128)}), f32[8,1,128]{2,1,0:T(1,128)S(1)}, u32[]{:S(2)}, u32[]{:S(2)}) async-start(f32[8,1,128]{2,1,0:T(1,128)} %bitcast.13), calls=%async_computation.4 | async-start | bytes 8192 | tf_op jit(solution)/shard_map/all_to_all | solution.py:67
  136.6 93.2 %reduce-scatter.6.cloned.1.call-start = ((), (), s32[]{:S(2)}) async-start(), calls=%async_computation.6 | async-start | bytes 110592
  172.6 0.6 copy-start
  229.8 7.1 %all-to-all-start.2 = ((f32[24,1,128]{2,1,0:T(1,128)}), f32[24,1,128]{2,1,0:T(1,128)S(1)}, u32[]{:S(2)}, u32[]{:S(2)}) async-start(f32[24,1,128]{2,1,0:T(1,128)} %bitcast.140), calls=%async_computation.2 | async-start | bytes 24576 | tf_op jit(solution)/shard_map/all_to_all | solution.py:66
Sparse Core Ops, SparseCore 0:
  173.4 56.4 reduce-scatter.5
